TPU v7x, 32 devices: a whole 2x2x4 slice. The times are simulated.
32 devices in a mesh: gx: 4 (over x, core), gy: 4 (over z), gz: 2 (over y).
Axes of the slice: x: 2, y: 2, z: 4, core: 2. Of those that a mesh axis runs over, the one named last changes fastest.
Arguments:
- kappa: float32 [5, 5, 5, 4, 4, 128], P(None, None, None, 'gx', 'gy', 'gz'), may hold values from 0.2 to 5
- source: float32 [5, 5, 5, 4, 4, 128], P(None, None, None, 'gx', 'gy', 'gz'), may hold values from -24 to 24
Outputs:
- solution: float32 [16, 16, 512], P('gx', 'gy', 'gz')
- residual: float32 [16, 16, 512], P('gx', 'gy', 'gz')
All inputs are finite; a program needn't handle non-finite values.
Results may differ from a plain program's by a relative error of at most 0.0003.
Values sent between devices are 32-bit elements; how exact they have to be, the bound alone decides.
A program may use at most 64 MiB of HBM per device.

v0:
```python
import math

import jax
import jax.numpy as jnp
import numpy as np
from jax import lax
from jax.sharding import PartitionSpec as P

LEVELS = 3


relax_weight = 0.6


def extended(cells, sides, width):
    for axis, dim in sides:
        count = lax.axis_size(axis)
        ends = count - 1
        head = lax.slice_in_dim(cells, 0, width, axis=dim)
        tail = lax.slice_in_dim(cells, cells.shape[dim] - width, cells.shape[dim], axis=dim)
        cells = jnp.concatenate(
            [
                lax.ppermute(tail, axis, [(i, (i + 1) % count) for i in range(ends)]),
                cells,
                lax.ppermute(head, axis, [((i + 1) % count, i) for i in range(ends)]),
            ],
            axis=dim,
        )
    return cells


def gll_tables():
    points = np.array([-1.0, -math.sqrt(3.0 / 7.0), 0.0, math.sqrt(3.0 / 7.0), 1.0])
    quad_weights = np.array([0.1, 49.0 / 90.0, 32.0 / 45.0, 49.0 / 90.0, 0.1])
    bary = np.array(
        [np.prod([points[i] - points[k] for k in range(5) if k != i]) for i in range(5)]
    )
    deriv = np.zeros((5, 5))
    for i in range(5):
        for j in range(5):
            if i != j:
                deriv[i, j] = bary[i] / (bary[j] * (points[i] - points[j]))
    for i in range(5):
        deriv[i, i] = -np.sum(deriv[i])
    return (
        jnp.asarray(points, jnp.float32),
        jnp.asarray(quad_weights, jnp.float32),
        jnp.asarray(deriv, jnp.float32),
    )


def split_first(values):
    count = (values.shape[0] - 1) // 4
    lower = jnp.swapaxes(values[:-1].reshape((count, 4) + values.shape[1:]), 0, 1)
    return jnp.concatenate([lower, values[4::4][None]], axis=0)


def merge_first(block):
    count = block.shape[1]
    rest = block.shape[2:]
    lower = jnp.swapaxes(block[:4], 0, 1).reshape((4 * count,) + rest)
    tail = jnp.concatenate([jnp.zeros((count, 3) + rest, block.dtype), block[4][:, None]], axis=1)
    tail = tail.reshape((4 * count,) + rest)
    spare = [(0, 0)] * len(rest)
    return jnp.pad(lower, [(0, 1)] + spare) + jnp.pad(tail, [(1, 0)] + spare)


def element_view(field):
    element_portion = split_first(field)
    element_portion = split_first(jnp.moveaxis(element_portion, 2, 0))
    element_portion = split_first(jnp.moveaxis(element_portion, 4, 0))
    return jnp.transpose(element_portion, (4, 2, 0, 5, 3, 1))


def node_sum(block):
    element_portion = jnp.transpose(block, (2, 5, 1, 4, 0, 3))
    element_portion = jnp.moveaxis(merge_first(element_portion), 0, 4)
    element_portion = jnp.moveaxis(merge_first(element_portion), 0, 2)
    return merge_first(element_portion)


def stiffness_terms(field, weighted, deriv):
    highest = lax.Precision.HIGHEST
    local = element_view(field)
    grad_x = jnp.einsum("ia,abcxyz->ibcxyz", deriv, local, precision=highest)
    grad_y = jnp.einsum("jb,abcxyz->ajcxyz", deriv, local, precision=highest)
    grad_z = jnp.einsum("kc,abcxyz->abkxyz", deriv, local, precision=highest)
    back = jnp.einsum("ia,ibcxyz->abcxyz", deriv, weighted * grad_x, precision=highest)
    back = back + jnp.einsum("jb,ajcxyz->abcxyz", deriv, weighted * grad_y, precision=highest)
    back = back + jnp.einsum("kc,abkxyz->abcxyz", deriv, weighted * grad_z, precision=highest)
    return node_sum(back)


def mass_pair(paired, width):
    return jnp.stack(
        [width / 6.0 * (2.0 * paired[0] + paired[1]), width / 6.0 * (paired[0] + 2.0 * paired[1])]
    )


def stiff_pair(paired, width):
    slope = (paired[0] - paired[1]) / width
    return jnp.stack([slope, -slope])


def lor_terms(field, coeff, spacing):
    width_x, width_y, width_z = spacing
    zpairs = jnp.stack([field[:, :, :-1], field[:, :, 1:]])
    zmass = mass_pair(zpairs, width_z)
    stiffness_along_z = stiff_pair(zpairs, width_z)
    ymass = jnp.stack([zmass[:, :, :-1], zmass[:, :, 1:]])
    ystiff = jnp.stack([stiffness_along_z[:, :, :-1], stiffness_along_z[:, :, 1:]])
    column_y = width_y[:, None]
    first = mass_pair(ymass, column_y)
    second = stiff_pair(ymass, column_y) + mass_pair(ystiff, column_y)
    column_x = width_x[:, None, None]
    xfirst = jnp.stack([first[:, :, :-1], first[:, :, 1:]])
    xsecond = jnp.stack([second[:, :, :-1], second[:, :, 1:]])
    cells = (stiff_pair(xfirst, column_x) + mass_pair(xsecond, column_x)) * coeff
    total = jnp.zeros(field.shape, jnp.float32)
    for a in range(2):
        for b in range(2):
            for c in range(2):
                total = total + jnp.pad(cells[a, b, c], ((a, 1 - a), (b, 1 - b), (c, 1 - c)))
    return total


def lor_diagonal(coeff, spacing):
    width_x = spacing[0][:, None, None]
    width_y = spacing[1][None, :, None]
    width_z = spacing[2][None, None, :]
    cells = coeff * (
        width_y * width_z / (9.0 * width_x)
        + width_x * width_z / (9.0 * width_y)
        + width_x * width_y / (9.0 * width_z)
    )
    shape = tuple((n + 1 for n in coeff.shape))
    total = jnp.zeros(shape, jnp.float32)
    for a in range(2):
        for b in range(2):
            for c in range(2):
                total = total + jnp.pad(cells, ((a, 1 - a), (b, 1 - b), (c, 1 - c)))
    return total


def subcell_coefficient(kappa):
    averaged = 0.5 * (kappa[:-1] + kappa[1:])
    averaged = 0.5 * (averaged[:, :-1] + averaged[:, 1:])
    averaged = 0.5 * (averaged[:, :, :-1] + averaged[:, :, 1:])
    count_x, count_y, count_z = averaged.shape[3:]
    return jnp.transpose(averaged, (3, 0, 4, 1, 5, 2)).reshape(
        4 * count_x, 4 * count_y, 4 * count_z
    )


def coarsen(coeff):
    nx, ny, nz = coeff.shape
    return jnp.mean(coeff.reshape(nx // 2, 2, ny // 2, 2, nz // 2, 2), axis=(1, 3, 5))


def interp_weights(width):
    paired = width.reshape(-1, 2)
    span = paired[:, 0] + paired[:, 1]
    return (paired[:, 1] / span, paired[:, 0] / span)


def prolong_first(coarse, left, right):
    shape = (-1,) + (1,) * (coarse.ndim - 1)
    middle = left.reshape(shape) * coarse[:-1] + right.reshape(shape) * coarse[1:]
    woven = jnp.stack([coarse[:-1], middle], axis=1).reshape(
        (2 * (coarse.shape[0] - 1),) + coarse.shape[1:]
    )
    return jnp.concatenate([woven, coarse[-1:]], axis=0)


def restrict_first(fine, left, right):
    shape = (-1,) + (1,) * (fine.ndim - 1)
    middle = fine[1::2]
    spare = [(0, 0)] * (fine.ndim - 1)
    return (
        fine[0::2]
        + jnp.pad(left.reshape(shape) * middle, [(0, 1)] + spare)
        + jnp.pad(right.reshape(shape) * middle, [(1, 0)] + spare)
    )


def prolong(coarse, weight_sets):
    for axis in range(3):
        left, right = weight_sets[axis]
        coarse = jnp.moveaxis(prolong_first(jnp.moveaxis(coarse, axis, 0), left, right), 0, axis)
    return coarse


def restrict(fine, weight_sets):
    for axis in range(3):
        left, right = weight_sets[axis]
        fine = jnp.moveaxis(restrict_first(jnp.moveaxis(fine, axis, 0), left, right), 0, axis)
    return fine


def collapse_leading(padded):
    inner = padded[1:-1]
    head = inner[0] + padded[0]
    tail = inner[-1] + padded[-1]
    return jnp.concatenate([head[None], inner[1:-1], tail[None]], axis=0)


def fold_axis(padded, axis):
    return jnp.moveaxis(collapse_leading(jnp.moveaxis(padded, axis, 0)), 0, axis)


def assemble(partial_value):
    padded = extended(partial_value, (("gx", 0), ("gy", 1), ("gz", 2)), 1)
    return fold_axis(fold_axis(fold_axis(padded, 0), 1), 2)


def side_mask(cells, position, devices):
    index = position * cells + jnp.arange(cells + 1)
    return ((index > 0) & (index < cells * devices)).astype(jnp.float32)


def block_mask(shape):
    mask_x = side_mask(shape[0], lax.axis_index("gx"), lax.axis_size("gx"))
    mask_y = side_mask(shape[1], lax.axis_index("gy"), lax.axis_size("gy"))
    mask_z = side_mask(shape[2], lax.axis_index("gz"), lax.axis_size("gz"))
    return mask_x[:, None, None] * mask_y[None, :, None] * mask_z[None, None, :]


def owned_mask(shape):
    sides = [(jnp.arange(n + 1) >= 1).astype(jnp.float32) for n in shape]
    return sides[0][:, None, None] * sides[1][None, :, None] * sides[2][None, None, :]


def cycle(level, forcing, levels):
    coeff, spacing, diag, mask, weight_sets, owned = levels[level]
    guess = relax_weight * forcing / diag
    if level == LEVELS - 1:
        guess = (
            guess
            + relax_weight * (forcing - mask * assemble(lor_terms(guess, coeff, spacing))) / diag
        )
        return guess
    defect = forcing * owned - lor_terms(guess, coeff, spacing)
    coarse = levels[level + 1][3] * assemble(restrict(defect, weight_sets))
    guess = guess + prolong(cycle(level + 1, coarse, levels), weight_sets)
    return (
        guess + relax_weight * (forcing - mask * assemble(lor_terms(guess, coeff, spacing))) / diag
    )


def inner_pair(resid, precond, image):
    local_rho = jnp.sum(resid[1:, 1:, 1:] * precond[1:, 1:, 1:])
    local_curv = jnp.sum(precond[1:, 1:, 1:] * image[1:, 1:, 1:])
    return lax.psum((local_rho, local_curv), ("gx", "gy", "gz"))


def body(kappa, source):
    points, quad_weights, deriv = gll_tables()
    cube = (
        quad_weights[:, None, None] * quad_weights[None, :, None] * quad_weights[None, None, :]
    ).reshape(5, 5, 5, 1, 1, 1)
    weighted = kappa * cube
    counts = kappa.shape[3:]
    finest_mask = block_mask([4 * c for c in counts])
    rhs = finest_mask * assemble(node_sum(cube * source))
    gaps = points[1:] - points[:-1]
    spacing = [jnp.tile(gaps, c) for c in counts]
    coeff = subcell_coefficient(kappa)
    levels = []
    for level in range(LEVELS):
        weight_sets = [interp_weights(h) for h in spacing] if level < LEVELS - 1 else None
        diag = assemble(lor_diagonal(coeff, spacing))
        levels.append(
            (coeff, spacing, diag, block_mask(coeff.shape), weight_sets, owned_mask(coeff.shape))
        )
        if level < LEVELS - 1:
            coeff = coarsen(coeff)
            spacing = [h.reshape(-1, 2).sum(axis=1) for h in spacing]

    def operator(field):
        return finest_mask * assemble(stiffness_terms(field, weighted, deriv))

    resid = rhs
    precond = cycle(0, resid, levels)
    image = operator(precond)
    rho_old, curv = inner_pair(resid, precond, image)
    alpha = rho_old / curv
    direction, along = (precond, image)
    iterate = alpha * direction
    resid = resid - alpha * along
    precond = cycle(0, resid, levels)
    image = operator(precond)
    rho_new, curv = inner_pair(resid, precond, image)
    ratio = rho_new / rho_old
    alpha = rho_new / (curv - ratio * rho_new / alpha)
    direction = precond + ratio * direction
    along = image + ratio * along
    iterate = iterate + alpha * direction
    resid = resid - alpha * along
    return (iterate[1:, 1:, 1:], resid[1:, 1:, 1:])


def solution(mesh):
    placed = (P(None, None, None, "gx", "gy", "gz"), P(None, None, None, "gx", "gy", "gz"))
    return jax.shard_map(
        body,
        mesh=mesh,
        in_specs=placed,
        out_specs=(P("gx", "gy", "gz"), P("gx", "gy", "gz")),
        check_vma=False,
    )
```

profile of v0, /device:TPU:0, one launch (start us, length us, event | category | flops | bytes accessed | tf_op | source)
XLA Modules:
  0.0 476.5 jit_solution(2688961487254693226)
XLA Ops:
  7.3 5.1 %collective-permute-start.18 = (f32[1,3,129]{2,1,0:T(4,128)S(1)}, f32[1,3,129]{2,1,0:T(4,128)S(1)}, u32[]{:S(2)}, u32[]{:S(2)}) collective-permute-start(f32[1,3,129]{2,1,0:T(4,128)S(1)} %get-tuple-element.387), channel_id=1, source_target_pairs={{0,8},{8,16},{16,24},{1,9},{9,17},{17,25},{2,10},{10,18},{18,26},{... | collective-permute-start | bytes 4652 | tf_op jit(solution)/shard_map/ppermute | solution.py:23
  65.5 4.5 collective-permute-start.2
  95.9 4.5 collective-permute-start.14
  109.1 4.2 collective-permute-done.17
  131.9 4.2 collective-permute-done.29
  139.5 4.2 collective-permute-done.37
  147.0 4.2 collective-permute-done.39
  154.2 4.2 collective-permute-done.41
  162.5 4.2 collective-permute-done.43
  169.9 4.2 collective-permute-done.45
  177.3 4.2 collective-permute-done.47
  188.7 4.2 collective-permute-done.49
  196.2 4.2 collective-permute-done.51
  203.7 4.2 collective-permute-done.53
  226.5 4.2 collective-permute-done.57
  234.0 4.2 collective-permute-done.59
  239.6 38.3 %all-reduce.156 = (f32[]{:T(128)}, f32[]{:T(128)}) all-reduce(f32[]{:T(128)} %get-tuple-element.13, f32[]{:T(128)} %get-tuple-element.12), channel_id=1, replica_groups=mesh['gx'=4,'gy'=4,'gz'=2] {'gx','gy','gz'}, use_global_device_ids=true, to_apply=%region_6.7 | all-reduce | flops 2 | bytes 16 | tf_op jit(solution)/shard_map/psum | solution.py:253
  283.7 4.3 collective-permute-done.61
  293.2 4.2 collective-permute-done.63
  303.0 4.2 collective-permute-done.65
  319.2 4.2 collective-permute-done.69
  326.4 4.2 collective-permute-done.71
  341.5 4.2 collective-permute-done.75
  348.8 4.2 collective-permute-done.77
  357.0 4.2 collective-permute-done.79
  364.5 4.2 collective-permute-done.81
  381.9 4.2 collective-permute-done.85
  389.4 4.2 collective-permute-done.87
  396.9 4.2 collective-permute-done.89
  419.0 4.2 collective-permute-done.93
  426.5 4.2 collective-permute-done.95
  432.2 38.3 %all-reduce.155 = (f32[]{:T(128)}, f32[]{:T(128)}) all-reduce(f32[]{:T(128)} %get-tuple-element.11, f32[]{:T(128)} %get-tuple-element.10), channel_id=1, replica_groups=mesh['gx'=4,'gy'=4,'gz'=2] {'gx','gy','gz'}, use_global_device_ids=true, to_apply=%region_10.11 | all-reduce | flops 2 | bytes 16 | tf_op jit(solution)/shard_map/psum | solution.py:253
  (746 shorter events, 262.1 us)
Async XLA Ops:
  3.1 57.5 %collective-permute-start.6 = (f32[1,5,257]{2,1,0:T(8,128)S(1)}, f32[1,5,257]{2,1,0:T(8,128)S(1)}, u32[]{:S(2)}, u32[]{:S(2)}) collective-permute-start(f32[1,5,257]{2,1,0:T(8,128)S(1)} %get-tuple-element.233), channel_id=1, source_target_pairs={{0,8},{8,16},{16,24},{1,9},{9,17},{17,25},{2,10},{10,18},{18,26},{... | collective-permute-start | bytes 15428 | tf_op jit(solution)/shard_map/ppermute | solution.py:23
  5.5 55.1 %collective-permute-start.7 = (f32[1,5,257]{2,1,0:T(8,128)S(1)}, f32[1,5,257]{2,1,0:T(8,128)S(1)}, u32[]{:S(2)}, u32[]{:S(2)}) collective-permute-start(f32[1,5,257]{2,1,0:T(8,128)S(1)} %get-tuple-element.234), channel_id=1, source_target_pairs={{8,0},{16,8},{24,16},{9,1},{17,9},{25,17},{10,2},{18,10},{26,18},{... | collective-permute-start | bytes 15428 | tf_op jit(solution)/shard_map/ppermute | solution.py:25
  7.3 20.0 %collective-permute-start.18 = (f32[1,3,129]{2,1,0:T(4,128)S(1)}, f32[1,3,129]{2,1,0:T(4,128)S(1)}, u32[]{:S(2)}, u32[]{:S(2)}) collective-permute-start(f32[1,3,129]{2,1,0:T(4,128)S(1)} %get-tuple-element.387), channel_id=1, source_target_pairs={{0,8},{8,16},{16,24},{1,9},{9,17},{17,25},{2,10},{10,18},{18,26},{... | collective-permute-start | bytes 4652 | tf_op jit(solution)/shard_map/ppermute | solution.py:23
  12.8 9.5 %collective-permute-start.30 = (f32[1,2,65]{2,1,0:T(2,128)S(1)}, f32[1,2,65]{2,1,0:T(2,128)S(1)}, u32[]{:S(2)}, u32[]{:S(2)}) collective-permute-start(f32[1,2,65]{2,1,0:T(2,128)S(1)} %get-tuple-element.509), channel_id=1, source_target_pairs={{0,8},{8,16},{16,24},{1,9},{9,17},{17,25},{2,10},{10,18},{18,26},{... | collective-permute-start | bytes 1568 | tf_op jit(solution)/shard_map/ppermute | solution.py:23
  16.5 7.2 %collective-permute-start.31 = (f32[1,2,65]{2,1,0:T(2,128)S(1)}, f32[1,2,65]{2,1,0:T(2,128)S(1)}, u32[]{:S(2)}, u32[]{:S(2)}) collective-permute-start(f32[1,2,65]{2,1,0:T(2,128)S(1)} %get-tuple-element.510), channel_id=1, source_target_pairs={{8,0},{16,8},{24,16},{9,1},{17,9},{25,17},{10,2},{18,10},{26,18},{... | collective-permute-start | bytes 1568 | tf_op jit(solution)/shard_map/ppermute | solution.py:25
  22.3 8.5 %collective-permute-start.19 = (f32[1,3,129]{2,1,0:T(4,128)S(1)}, f32[1,3,129]{2,1,0:T(4,128)S(1)}, u32[]{:S(2)}, u32[]{:S(2)}) collective-permute-start(f32[1,3,129]{2,1,0:T(4,128)S(1)} %get-tuple-element.388), channel_id=1, source_target_pairs={{8,0},{16,8},{24,16},{9,1},{17,9},{25,17},{10,2},{18,10},{26,18},{... | collective-permute-start | bytes 4652 | tf_op jit(solution)/shard_map/ppermute | solution.py:25
  23.6 41.8 %collective-permute-start = (f32[1,5,257]{2,1,0:T(8,128)S(1)}, f32[1,5,257]{2,1,0:T(8,128)S(1)}, u32[]{:S(2)}, u32[]{:S(2)}) collective-permute-start(f32[1,5,257]{2,1,0:T(8,128)S(1)} %get-tuple-element.131), channel_id=1, source_target_pairs={{0,8},{8,16},{16,24},{1,9},{9,17},{17,25},{2,10},{10,18},{18,26},{... | collective-permute-start | bytes 15428 | tf_op jit(solution)/shard_map/ppermute | solution.py:23
  41.2 5.6 %collective-permute-start.20 = (f32[5,1,129]{2,1,0:T(1,128)S(1)}, f32[5,1,129]{2,1,0:T(1,128)S(1)}, u32[]{:S(2)}, u32[]{:S(2)}) collective-permute-start(f32[5,1,129]{2,1,0:T(1,128)S(1)} %get-tuple-element.289), channel_id=1, source_target_pairs={{0,2},{2,4},{4,6},{1,3},{3,5},{5,7},{8,10},{10,12},{12,14},{9,11},... | collective-permute-start | bytes 7748 | tf_op jit(solution)/shard_map/ppermute | solution.py:23
  54.7 5.7 %collective-permute-start.23 = (f32[5,5,1]{2,1,0:T(8,128)S(1)}, f32[5,5,1]{2,1,0:T(8,128)S(1)}, u32[]{:S(2)}, u32[]{:S(2)}) collective-permute-start(f32[5,5,1]{2,1,0:T(8,128)S(1)} %get-tuple-element.258), channel_id=1, source_target_pairs={{1,0},{3,2},{5,4},{7,6},{9,8},{11,10},{13,12},{15,14},{17,16},{19,... | collective-permute-start | bytes 308 | tf_op jit(solution)/shard_map/ppermute | solution.py:25
  56.2 9.2 %collective-permute-start.1 = (f32[1,5,257]{2,1,0:T(8,128)S(1)}, f32[1,5,257]{2,1,0:T(8,128)S(1)}, u32[]{:S(2)}, u32[]{:S(2)}) collective-permute-start(f32[1,5,257]{2,1,0:T(8,128)S(1)} %get-tuple-element.132), channel_id=1, source_target_pairs={{8,0},{16,8},{24,16},{9,1},{17,9},{25,17},{10,2},{18,10},{26,18},{... | collective-permute-start | bytes 15428 | tf_op jit(solution)/shard_map/ppermute | solution.py:25
  60.6 10.7 %collective-permute-start.8 = (f32[7,1,257]{2,1,0:T(1,128)S(1)}, f32[7,1,257]{2,1,0:T(1,128)S(1)}, u32[]{:S(2)}, u32[]{:S(2)}) collective-permute-start(f32[7,1,257]{2,1,0:T(1,128)S(1)} %get-tuple-element.143), channel_id=1, source_target_pairs={{0,2},{2,4},{4,6},{1,3},{3,5},{5,7},{8,10},{10,12},{12,14},{9,11},... | collective-permute-start | bytes 21596 | tf_op jit(solution)/shard_map/ppermute | solution.py:23
  64.1 7.2 %collective-permute-start.9 = (f32[7,1,257]{2,1,0:T(1,128)S(1)}, f32[7,1,257]{2,1,0:T(1,128)S(1)}, u32[]{:S(2)}, u32[]{:S(2)}) collective-permute-start(f32[7,1,257]{2,1,0:T(1,128)S(1)} %get-tuple-element.144), channel_id=1, source_target_pairs={{2,0},{4,2},{6,4},{3,1},{5,3},{7,5},{10,8},{12,10},{14,12},{11,9},... | collective-permute-start | bytes 21596 | tf_op jit(solution)/shard_map/ppermute | solution.py:25
  65.5 8.9 %collective-permute-start.2 = (f32[7,1,257]{2,1,0:T(1,128)S(1)}, f32[7,1,257]{2,1,0:T(1,128)S(1)}, u32[]{:S(2)}, u32[]{:S(2)}) collective-permute-start(f32[7,1,257]{2,1,0:T(1,128)S(1)} %get-tuple-element.141), channel_id=1, source_target_pairs={{0,2},{2,4},{4,6},{1,3},{3,5},{5,7},{8,10},{10,12},{12,14},{9,11},... | collective-permute-start | bytes 21596 | tf_op jit(solution)/shard_map/ppermute | solution.py:23
  70.0 5.6 %collective-permute-start.3 = (f32[7,1,257]{2,1,0:T(1,128)S(1)}, f32[7,1,257]{2,1,0:T(1,128)S(1)}, u32[]{:S(2)}, u32[]{:S(2)}) collective-permute-start(f32[7,1,257]{2,1,0:T(1,128)S(1)} %get-tuple-element.142), channel_id=1, source_target_pairs={{2,0},{4,2},{6,4},{3,1},{5,3},{7,5},{10,8},{12,10},{14,12},{11,9},... | collective-permute-start | bytes 21596 | tf_op jit(solution)/shard_map/ppermute | solution.py:25
  71.4 8.9 %collective-permute-start.10 = (f32[7,7,1]{2,1,0:T(8,128)S(1)}, f32[7,7,1]{2,1,0:T(8,128)S(1)}, u32[]{:S(2)}, u32[]{:S(2)}) collective-permute-start(f32[7,7,1]{2,1,0:T(8,128)S(1)} %get-tuple-element.125), channel_id=1, source_target_pairs={{0,1},{2,3},{4,5},{6,7},{8,9},{10,11},{12,13},{14,15},{16,17},{18,... | collective-permute-start | bytes 596 | tf_op jit(solution)/shard_map/ppermute | solution.py:23
  73.0 7.2 %collective-permute-start.11 = (f32[7,7,1]{2,1,0:T(8,128)S(1)}, f32[7,7,1]{2,1,0:T(8,128)S(1)}, u32[]{:S(2)}, u32[]{:S(2)}) collective-permute-start(f32[7,7,1]{2,1,0:T(8,128)S(1)} %get-tuple-element.126), channel_id=1, source_target_pairs={{1,0},{3,2},{5,4},{7,6},{9,8},{11,10},{13,12},{15,14},{17,16},{19,... | collective-permute-start | bytes 596 | tf_op jit(solution)/shard_map/ppermute | solution.py:25
  78.9 5.8 %collective-permute-start.5 = (f32[7,7,1]{2,1,0:T(8,128)S(1)}, f32[7,7,1]{2,1,0:T(8,128)S(1)}, u32[]{:S(2)}, u32[]{:S(2)}) collective-permute-start(f32[7,7,1]{2,1,0:T(8,128)S(1)} %get-tuple-element.124), channel_id=1, source_target_pairs={{1,0},{3,2},{5,4},{7,6},{9,8},{11,10},{13,12},{15,14},{17,16},{19,... | collective-permute-start | bytes 596 | tf_op jit(solution)/shard_map/ppermute | solution.py:25
  95.9 5.9 %collective-permute-start.14 = (f32[5,1,129]{2,1,0:T(1,128)S(1)}, f32[5,1,129]{2,1,0:T(1,128)S(1)}, u32[]{:S(2)}, u32[]{:S(2)}) collective-permute-start(f32[5,1,129]{2,1,0:T(1,128)S(1)} %get-tuple-element.291), channel_id=1, source_target_pairs={{0,2},{2,4},{4,6},{1,3},{3,5},{5,7},{8,10},{10,12},{12,14},{9,11},... | collective-permute-start | bytes 7748 | tf_op jit(solution)/shard_map/ppermute | solution.py:23
  107.6 5.7 %collective-permute-start.17 = (f32[5,5,1]{2,1,0:T(8,128)S(1)}, f32[5,5,1]{2,1,0:T(8,128)S(1)}, u32[]{:S(2)}, u32[]{:S(2)}) collective-permute-start(f32[5,5,1]{2,1,0:T(8,128)S(1)} %get-tuple-element.263), channel_id=1, source_target_pairs={{1,0},{3,2},{5,4},{7,6},{9,8},{11,10},{13,12},{15,14},{17,16},{19,... | collective-permute-start | bytes 308 | tf_op jit(solution)/shard_map/ppermute | solution.py:25
  175.8 5.7 %collective-permute-start.47 = (f32[5,5,1]{2,1,0:T(8,128)S(1)}, f32[5,5,1]{2,1,0:T(8,128)S(1)}, u32[]{:S(2)}, u32[]{:S(2)}) collective-permute-start(f32[5,5,1]{2,1,0:T(8,128)S(1)} %get-tuple-element.253), channel_id=1, source_target_pairs={{1,0},{3,2},{5,4},{7,6},{9,8},{11,10},{13,12},{15,14},{17,16},{19,... | collective-permute-start | bytes 308 | tf_op jit(solution)/shard_map/ppermute | solution.py:25
  187.2 5.7 %collective-permute-start.49 = (f32[1,5,257]{2,1,0:T(8,128)S(1)}, f32[1,5,257]{2,1,0:T(8,128)S(1)}, u32[]{:S(2)}, u32[]{:S(2)}) collective-permute-start(f32[1,5,257]{2,1,0:T(8,128)S(1)} %get-tuple-element.218), channel_id=1, source_target_pairs={{8,0},{16,8},{24,16},{9,1},{17,9},{25,17},{10,2},{18,10},{26,18},{... | collective-permute-start | bytes 15428 | tf_op jit(solution)/shard_map/ppermute | solution.py:25
  194.8 5.6 %collective-permute-start.51 = (f32[7,1,257]{2,1,0:T(1,128)S(1)}, f32[7,1,257]{2,1,0:T(1,128)S(1)}, u32[]{:S(2)}, u32[]{:S(2)}) collective-permute-start(f32[7,1,257]{2,1,0:T(1,128)S(1)} %get-tuple-element.140), channel_id=1, source_target_pairs={{2,0},{4,2},{6,4},{3,1},{5,3},{7,5},{10,8},{12,10},{14,12},{11,9},... | collective-permute-start | bytes 21596 | tf_op jit(solution)/shard_map/ppermute | solution.py:25
  202.1 5.8 %collective-permute-start.53 = (f32[7,7,1]{2,1,0:T(8,128)S(1)}, f32[7,7,1]{2,1,0:T(8,128)S(1)}, u32[]{:S(2)}, u32[]{:S(2)}) collective-permute-start(f32[7,7,1]{2,1,0:T(8,128)S(1)} %get-tuple-element.122), channel_id=1, source_target_pairs={{1,0},{3,2},{5,4},{7,6},{9,8},{11,10},{13,12},{15,14},{17,16},{19,... | collective-permute-start | bytes 596 | tf_op jit(solution)/shard_map/ppermute | solution.py:25
  225.1 5.6 %collective-permute-start.57 = (f32[7,1,257]{2,1,0:T(1,128)S(1)}, f32[7,1,257]{2,1,0:T(1,128)S(1)}, u32[]{:S(2)}, u32[]{:S(2)}) collective-permute-start(f32[7,1,257]{2,1,0:T(1,128)S(1)} %get-tuple-element.138), channel_id=1, source_target_pairs={{2,0},{4,2},{6,4},{3,1},{5,3},{7,5},{10,8},{12,10},{14,12},{11,9},... | collective-permute-start | bytes 21596 | tf_op jit(solution)/shard_map/ppermute | solution.py:25
  232.4 5.8 %collective-permute-start.59 = (f32[7,7,1]{2,1,0:T(8,128)S(1)}, f32[7,7,1]{2,1,0:T(8,128)S(1)}, u32[]{:S(2)}, u32[]{:S(2)}) collective-permute-start(f32[7,7,1]{2,1,0:T(8,128)S(1)} %get-tuple-element.120), channel_id=1, source_target_pairs={{1,0},{3,2},{5,4},{7,6},{9,8},{11,10},{13,12},{15,14},{17,16},{19,... | collective-permute-start | bytes 596 | tf_op jit(solution)/shard_map/ppermute | solution.py:25
  282.4 5.6 %collective-permute-start.61 = (f32[1,3,129]{2,1,0:T(4,128)S(1)}, f32[1,3,129]{2,1,0:T(4,128)S(1)}, u32[]{:S(2)}, u32[]{:S(2)}) collective-permute-start(f32[1,3,129]{2,1,0:T(4,128)S(1)} %get-tuple-element.356), channel_id=1, source_target_pairs={{8,0},{16,8},{24,16},{9,1},{17,9},{25,17},{10,2},{18,10},{26,18},{... | collective-permute-start | bytes 4652 | tf_op jit(solution)/shard_map/ppermute | solution.py:25
  297.4 5.6 %collective-permute-start.64 = (f32[5,5,1]{2,1,0:T(8,128)S(1)}, f32[5,5,1]{2,1,0:T(8,128)S(1)}, u32[]{:S(2)}, u32[]{:S(2)}) collective-permute-start(f32[5,5,1]{2,1,0:T(8,128)S(1)} %get-tuple-element.245), channel_id=1, source_target_pairs={{0,1},{2,3},{4,5},{6,7},{8,9},{10,11},{12,13},{14,15},{16,17},{18,... | collective-permute-start | bytes 308 | tf_op jit(solution)/shard_map/ppermute | solution.py:23
  301.5 5.7 %collective-permute-start.65 = (f32[5,5,1]{2,1,0:T(8,128)S(1)}, f32[5,5,1]{2,1,0:T(8,128)S(1)}, u32[]{:S(2)}, u32[]{:S(2)}) collective-permute-start(f32[5,5,1]{2,1,0:T(8,128)S(1)} %get-tuple-element.246), channel_id=1, source_target_pairs={{1,0},{3,2},{5,4},{7,6},{9,8},{11,10},{13,12},{15,14},{17,16},{19,... | collective-permute-start | bytes 308 | tf_op jit(solution)/shard_map/ppermute | solution.py:25
  370.3 5.7 %collective-permute-start.83 = (f32[5,5,1]{2,1,0:T(8,128)S(1)}, f32[5,5,1]{2,1,0:T(8,128)S(1)}, u32[]{:S(2)}, u32[]{:S(2)}) collective-permute-start(f32[5,5,1]{2,1,0:T(8,128)S(1)} %get-tuple-element.241), channel_id=1, source_target_pairs={{1,0},{3,2},{5,4},{7,6},{9,8},{11,10},{13,12},{15,14},{17,16},{19,... | collective-permute-start | bytes 308 | tf_op jit(solution)/shard_map/ppermute | solution.py:25
  388.0 5.6 %collective-permute-start.87 = (f32[7,1,257]{2,1,0:T(1,128)S(1)}, f32[7,1,257]{2,1,0:T(1,128)S(1)}, u32[]{:S(2)}, u32[]{:S(2)}) collective-permute-start(f32[7,1,257]{2,1,0:T(1,128)S(1)} %get-tuple-element.136), channel_id=1, source_target_pairs={{2,0},{4,2},{6,4},{3,1},{5,3},{7,5},{10,8},{12,10},{14,12},{11,9},... | collective-permute-start | bytes 21596 | tf_op jit(solution)/shard_map/ppermute | solution.py:25
  395.3 5.8 %collective-permute-start.89 = (f32[7,7,1]{2,1,0:T(8,128)S(1)}, f32[7,7,1]{2,1,0:T(8,128)S(1)}, u32[]{:S(2)}, u32[]{:S(2)}) collective-permute-start(f32[7,7,1]{2,1,0:T(8,128)S(1)} %get-tuple-element.118), channel_id=1, source_target_pairs={{1,0},{3,2},{5,4},{7,6},{9,8},{11,10},{13,12},{15,14},{17,16},{19,... | collective-permute-start | bytes 596 | tf_op jit(solution)/shard_map/ppermute | solution.py:25
  424.9 5.8 %collective-permute-start.95 = (f32[7,7,1]{2,1,0:T(8,128)S(1)}, f32[7,7,1]{2,1,0:T(8,128)S(1)}, u32[]{:S(2)}, u32[]{:S(2)}) collective-permute-start(f32[7,7,1]{2,1,0:T(8,128)S(1)} %get-tuple-element.116), channel_id=1, source_target_pairs={{1,0},{3,2},{5,4},{7,6},{9,8},{11,10},{13,12},{15,14},{17,16},{19,... | collective-permute-start | bytes 596 | tf_op jit(solution)/shard_map/ppermute | solution.py:25
  (85 other events, 288.2 us)
where the time goes:
time: 480 us; the launch traced here: 477 us
  starting transfers between devices  172 us (36%)
  waiting for transfers between devices  169 us (35%)
  blocking collectives  76.6 us (16%)
  local copies, waits for them, and re-layouts  27.5 us (6%)
  other arithmetic  17.6 us (4%)
  between operations  10.6 us (2%)
    ppermute x48, waiting for transfers between devices, extended(): lax.ppermute(head, axis, [((i + 1) % count, i) for i in range(ends)])  167 us
    ppermute x48, starting transfers between devices, extended(): lax.ppermute(tail, axis, [(i, (i + 1) % count) for i in range(ends)])  109 us
    psum x2, blocking collectives, inner_pair(): return lax.psum((local_rho, local_curv), ('gx', 'gy', 'gz'))  76.6 us
    ppermute x48, starting transfers between devices, extended(): lax.ppermute(head, axis, [((i + 1) % count, i) for i in range(ends)])  62.4 us
  transfers between devices with their start and end apart: 96, of which 54 were waited for; matrix products, arithmetic and copies ran while one was open for 1% of the time, Pallas kernels for 0%

commit v1 on v0

--- a/solution.py
+++ b/solution.py
@@ -4,6 +4,8 @@
 import jax.numpy as jnp
 import numpy as np
 from jax import lax
+from jax.experimental import pallas as pl
+from jax.experimental.pallas import tpu as pltpu
 from jax.sharding import PartitionSpec as P
 
 LEVELS = 3
@@ -253,7 +255,7 @@
     return lax.psum((local_rho, local_curv), ("gx", "gy", "gz"))
 
 
-def body(kappa, source):
+def distributed_body(kappa, source):
     points, quad_weights, deriv = gll_tables()
     cube = (
         quad_weights[:, None, None] * quad_weights[None, :, None] * quad_weights[None, None, :]
@@ -299,6 +301,504 @@
     return (iterate[1:, 1:, 1:], resid[1:, 1:, 1:])
 
 
+def host_tables():
+    points = np.array([-1.0, -math.sqrt(3.0 / 7.0), 0.0, math.sqrt(3.0 / 7.0), 1.0])
+    quad = np.array([0.1, 49.0 / 90.0, 32.0 / 45.0, 49.0 / 90.0, 0.1])
+    bary = np.array(
+        [np.prod([points[i] - points[k] for k in range(5) if k != i]) for i in range(5)]
+    )
+    deriv = np.zeros((5, 5))
+    for i in range(5):
+        for j in range(5):
+            if i != j:
+                deriv[i, j] = bary[i] / (bary[j] * (points[i] - points[j]))
+    for i in range(5):
+        deriv[i, i] = -np.sum(deriv[i])
+    deriv[2, 2] = 0.0
+    return points, quad, deriv
+
+
+POINTS, QUAD, DERIV = host_tables()
+GAPS = [float(v) for v in POINTS[1:] - POINTS[:-1]]
+WIDTHS = [GAPS]
+while len(WIDTHS) < LEVELS:
+    last = WIDTHS[-1]
+    WIDTHS.append([last[2 * i] + last[2 * i + 1] for i in range(len(last) // 2)])
+
+
+def apply_odd(matrix, u):
+    e0, e1, o0, o1 = u[0] + u[4], u[1] + u[3], u[0] - u[4], u[1] - u[3]
+    out = [None] * 5
+    for i in range(2):
+        row = matrix[i]
+        p = (
+            float(0.5 * (row[0] + row[4])) * e0
+            + float(0.5 * (row[1] + row[3])) * e1
+            + float(row[2]) * u[2]
+        )
+        q = float(0.5 * (row[0] - row[4])) * o0 + float(0.5 * (row[1] - row[3])) * o1
+        out[i] = q + p
+        out[4 - i] = q - p
+    out[2] = float(matrix[2][0]) * o0 + float(matrix[2][1]) * o1
+    return out
+
+
+def line_terms(u, w):
+    grad = apply_odd(DERIV, u)
+    return apply_odd(DERIV.T, [w[i] * grad[i] for i in range(5)])
+
+
+def plane_terms(v0, v1, coef, hx, inv_hx, widths):
+    n = len(widths)
+    quarter, twelfth = hx * 0.25, hx * (1.0 / 12.0)
+    cache = {}
+
+    def weights(hy, hz):
+        key = (round(hy, 12), round(hz, 12))
+        if key not in cache:
+            m = [[hy / 4 * hz / 4, hy / 4 * hz / 12], [hy / 12 * hz / 4, hy / 12 * hz / 12]]
+            k = [
+                [0.0, hy / 4 / hz],
+                [hz / 4 / hy, hz / 12 / hy + hy / 12 / hz],
+            ]
+            cache[key] = (
+                [[quarter * k[j][l] for l in range(2)] for j in range(2)],
+                [[inv_hx * m[j][l] + twelfth * k[j][l] for l in range(2)] for j in range(2)],
+            )
+        return cache[key]
+
+    near, far = {}, {}
+
+    def add(store, key, value):
+        store[key] = store[key] + value if key in store else value
+
+    sums = {k: v0[k] + v1[k] for k in v0}
+    diffs = {k: v0[k] - v1[k] for k in v0}
+    back = [{}, {}]
+    for b in range(n):
+        line = {}
+        for c in range(n):
+            for xi, field in ((0, sums), (1, diffs)):
+                lo, hi = (field[b, c], field[b + 1, c]), None
+                ys = []
+                for cc in (c, c + 1):
+                    key = (xi, cc)
+                    if key not in line:
+                        line[key] = (
+                            field[b, cc] + field[b + 1, cc],
+                            field[b, cc] - field[b + 1, cc],
+                        )
+        zline = {}
+        for c in range(n):
+            ws, wd = weights(widths[b], widths[c])
+            value = coef(b, c)
+            for xi, w in ((0, ws), (1, wd)):
+                for yi in range(2):
+                    left, right = line[xi, c][yi], line[xi, c + 1][yi]
+                    d = (w[yi][1] * value) * (left - right)
+                    if xi == 0 and yi == 0:
+                        add(zline, (xi, yi, c), d)
+                        add(zline, (xi, yi, c + 1), -d)
+                    else:
+                        s = (w[yi][0] * value) * (left + right)
+                        add(zline, (xi, yi, c), s + d)
+                        add(zline, (xi, yi, c + 1), s - d)
+        for c in range(n + 1):
+            for xi in range(2):
+                s, d = zline[xi, 0, c], zline[xi, 1, c]
+                add(back[xi], (b, c), s + d)
+                add(back[xi], (b + 1, c), s - d)
+    for key in back[0]:
+        near[key] = back[0][key] + back[1][key]
+        far[key] = back[0][key] - back[1][key]
+    return near, far
+
+
+def replicated_kernel(
+    ny, where_ref, kappa_ref, source_ref, solution_ref, residual_ref,
+    weighted, expanded, out, coeff, winv, resid, guess, direction, iterate,
+):
+    rows, lanes = kappa_ref.shape[3:]
+    halves = rows // 8
+
+    def next_x(t):
+        return pltpu.roll(t, rows - ny, 0)
+
+    def next_y(t):
+        return pltpu.roll(t, rows - 1, 0)
+
+    def next_z(t):
+        return pltpu.roll(t, lanes - 1, 1)
+
+    def prev_x(t):
+        return pltpu.roll(t, ny, 0)
+
+    def prev_y(t):
+        return pltpu.roll(t, 1, 0)
+
+    def prev_z(t):
+        return pltpu.roll(t, 1, 1)
+
+    row = lax.broadcasted_iota(jnp.int32, (rows, lanes), 0)
+    lane = lax.broadcasted_iota(jnp.int32, (rows, lanes), 1)
+    keep_x = (row >= ny).astype(jnp.float32)
+    keep_y = (lax.rem(row, ny) > 0).astype(jnp.float32)
+    keep_z = (lane > 0).astype(jnp.float32)
+
+    def masked(a, b, c, t):
+        if a == 0:
+            t = t * keep_x
+        if b == 0:
+            t = t * keep_y
+        if c == 0:
+            t = t * keep_z
+        return t
+
+    def phases(n):
+        return [(a, b, c) for a in range(n) for b in range(n) for c in range(n)]
+
+    def expand(n, get, put):
+        for a in range(n):
+            for b in range(n):
+                put((a, b, n), next_z(get((a, b, 0))))
+        for a in range(n):
+            for c in range(n + 1):
+                put((a, n, c), next_y(get((a, 0, c))))
+        for b in range(n + 1):
+            for c in range(n + 1):
+                put((n, b, c), next_x(get((0, b, c))))
+
+    def fold(n, get, put):
+        for b in range(n + 1):
+            for c in range(n + 1):
+                put((0, b, c), get((0, b, c)) + prev_x(get((n, b, c))))
+        for a in range(n):
+            for c in range(n + 1):
+                put((a, 0, c), get((a, 0, c)) + prev_y(get((a, n, c))))
+        for a in range(n):
+            for b in range(n):
+                put((a, b, 0), get((a, b, 0)) + prev_z(get((a, b, n))))
+
+    def put_in(ref):
+        def put(k, t):
+            ref[k] = t
+        return put
+
+    def get_from(ref):
+        return lambda k: ref[k]
+
+    for a in range(5):
+        for b in range(5):
+            for c in range(5):
+                w = float(QUAD[a] * QUAD[b] * QUAD[c])
+                weighted[a, b, c] = w * kappa_ref[a, b, c]
+                out[a, b, c] = w * source_ref[a, b, c]
+    fold(4, get_from(out), put_in(out))
+    for k in phases(4):
+        resid[k] = masked(*k, out[k])
+        direction[k] = jnp.zeros((rows, lanes), jnp.float32)
+        iterate[k] = jnp.zeros((rows, lanes), jnp.float32)
+
+    def pair_z(h):
+        i, _ = h
+        return i
+
+    for a in range(4):
+        two = {
+            (b, c): kappa_ref[a, b, c] + kappa_ref[a + 1, b, c]
+            for b in range(5) for c in range(5)
+        }
+        two = {(b, c): two[b, c] + two[b + 1, c] for b in range(4) for c in range(5)}
+        for b in range(4):
+            for c in range(4):
+                coeff[a, b, c] = 0.125 * (two[b, c] + two[b, c + 1])
+
+    def halved(n, get):
+        result = {}
+        for a, b, c in phases(n // 2):
+            t = None
+            for x in range(2):
+                for y in range(2):
+                    for z in range(2):
+                        v = get((2 * a + x, 2 * b + y, 2 * c + z))
+                        t = v if t is None else t + v
+            result[a, b, c] = 0.125 * t
+        return result
+
+    coeff1 = halved(4, get_from(coeff))
+    coeff2 = halved(2, coeff1.__getitem__)
+
+    def inverse_diagonal(n, widths, get, put):
+        cells = {}
+        for a, b, c in phases(n):
+            x, y, z = widths[a], widths[b], widths[c]
+            cells[a, b, c] = get((a, b, c)) * (
+                y * z / (9.0 * x) + x * z / (9.0 * y) + x * y / (9.0 * z)
+            )
+        for axis, prev in ((0, prev_x), (1, prev_y), (2, prev_z)):
+            sums = {}
+            for k in phases(n):
+                lower = list(k)
+                lower[axis] = (k[axis] - 1) % n
+                t = cells[tuple(lower)]
+                sums[k] = cells[k] + (prev(t) if k[axis] == 0 else t)
+            cells = sums
+        for k in phases(n):
+            put(k, masked(*k, relax_weight / cells[k]))
+
+    inverse_diagonal(4, WIDTHS[0], get_from(coeff), put_in(winv))
+    winv1, winv2 = {}, {}
+    inverse_diagonal(2, WIDTHS[1], coeff1.__getitem__, winv1.__setitem__)
+    inverse_diagonal(1, WIDTHS[2], coeff2.__getitem__, winv2.__setitem__)
+
+    def lor_fine():
+        expand(4, get_from(expanded), put_in(expanded))
+        for b in range(5):
+            for c in range(5):
+                out[0, b, c] = jnp.zeros((rows, lanes), jnp.float32)
+
+        def step(i, carry):
+            a = lax.rem(i, 4)
+            part = pl.ds(pl.multiple_of((i // 4) * 8, 8), 8)
+            outer = (a == 0) | (a == 3)
+            hx = jnp.where(outer, GAPS[0], GAPS[1])
+            inv_hx = jnp.where(outer, 1.0 / GAPS[0], 1.0 / GAPS[1])
+            keys = [(b, c) for b in range(5) for c in range(5)]
+            v0 = {k: expanded[a, k[0], k[1], part, :] for k in keys}
+            v1 = {k: expanded[a + 1, k[0], k[1], part, :] for k in keys}
+            near, far = plane_terms(
+                v0, v1, lambda b, c: coeff[a, b, c, part, :], hx, inv_hx, GAPS
+            )
+            for b, c in keys:
+                out[a, b, c, part, :] += near[b, c]
+                out[a + 1, b, c, part, :] = far[b, c]
+            return carry
+
+        lax.fori_loop(0, 4 * halves, step, 0)
+        fold(4, get_from(out), put_in(out))
+
+    def lor_coarse(field, n, widths, coefs):
+        v = dict(field)
+        expand(n, v.__getitem__, v.__setitem__)
+        total = {}
+        for a in range(n):
+            keys = [(b, c) for b in range(n + 1) for c in range(n + 1)]
+            near, far = plane_terms(
+                {k: v[(a,) + k] for k in keys},
+                {k: v[(a + 1,) + k] for k in keys},
+                lambda b, c: coefs[a, b, c],
+                widths[a],
+                1.0 / widths[a],
+                widths,
+            )
+            for k in keys:
+                key = (a,) + k
+                total[key] = total[key] + near[k] if key in total else near[k]
+                total[(a + 1,) + k] = far[k]
+        fold(n, total.__getitem__, total.__setitem__)
+        return total
+
+    def shares(widths):
+        left, right = [], []
+        for i in range(len(widths) // 2):
+            span = widths[2 * i] + widths[2 * i + 1]
+            left.append(widths[2 * i + 1] / span)
+            right.append(widths[2 * i] / span)
+        return left, right
+
+    def restrict_phases(field, n, widths):
+        left, right = shares(widths)
+        half = n // 2
+        sizes = [n, n, n]
+        for axis, prev in ((2, prev_z), (1, prev_y), (0, prev_x)):
+            sizes[axis] = half
+            coarse = {}
+            for a in range(sizes[0]):
+                for b in range(sizes[1]):
+                    for c in range(sizes[2]):
+                        k = (a, b, c)
+                        j = k[axis]
+
+                        def at(i):
+                            return field[k[:axis] + (i,) + k[axis + 1:]]
+
+                        if j == 0:
+                            before = right[half - 1] * prev(at(n - 1))
+                        else:
+                            before = right[j - 1] * at(2 * j - 1)
+                        coarse[k] = at(2 * j) + left[j] * at(2 * j + 1) + before
+            field = coarse
+        return field
+
+    def prolong_phases(field, n, widths):
+        left, right = shares(widths)
+        half = n // 2
+        sizes = [half, half, half]
+        for axis, following in ((0, next_x), (1, next_y), (2, next_z)):
+            sizes[axis] = n
+            fine = {}
+            for a in range(sizes[0]):
+                for b in range(sizes[1]):
+                    for c in range(sizes[2]):
+                        k = (a, b, c)
+                        i, odd = divmod(k[axis], 2)
+
+                        def at(j):
+                            return field[k[:axis] + (j,) + k[axis + 1:]]
+
+                        if odd:
+                            after = following(at(0)) if i + 1 == half else at(i + 1)
+                            fine[k] = left[i] * at(i) + right[i] * after
+                        else:
+                            fine[k] = at(i)
+            field = fine
+        return field
+
+    def precondition():
+        for k in phases(4):
+            t = winv[k] * resid[k]
+            guess[k] = t
+            expanded[k] = t
+        lor_fine()
+        defect = {k: resid[k] - out[k] for k in phases(4)}
+        f1 = restrict_phases(defect, 4, WIDTHS[0])
+        g1 = {k: winv1[k] * f1[k] for k in f1}
+        l1 = lor_coarse(g1, 2, WIDTHS[1], coeff1)
+        f2 = restrict_phases({k: f1[k] - l1[k] for k in f1}, 2, WIDTHS[1])
+        g2 = {k: winv2[k] * f2[k] for k in f2}
+        l2 = lor_coarse(g2, 1, WIDTHS[2], coeff2)
+        g2 = {k: g2[k] + winv2[k] * (f2[k] - l2[k]) for k in f2}
+        p1 = prolong_phases(g2, 2, WIDTHS[1])
+        g1 = {k: g1[k] + p1[k] for k in f1}
+        l1 = lor_coarse(g1, 2, WIDTHS[1], coeff1)
+        g1 = {k: g1[k] + winv1[k] * (f1[k] - l1[k]) for k in f1}
+        p0 = prolong_phases(g1, 4, WIDTHS[0])
+        for k in phases(4):
+            t = guess[k] + p0[k]
+            guess[k] = t
+            expanded[k] = t
+        lor_fine()
+
+    def operator():
+        expand(4, get_from(expanded), put_in(expanded))
+
+        def plane(i, carry):
+            a = lax.rem(i, 5)
+            part = pl.ds(pl.multiple_of((i // 5) * 8, 8), 8)
+            total = {}
+            u = {(b, c): expanded[a, b, c, part, :] for b in range(5) for c in range(5)}
+            w = {(b, c): weighted[a, b, c, part, :] for b in range(5) for c in range(5)}
+            for c in range(5):
+                y = line_terms([u[b, c] for b in range(5)], [w[b, c] for b in range(5)])
+                for b in range(5):
+                    total[b, c] = y[b]
+            for b in range(5):
+                y = line_terms([u[b, c] for c in range(5)], [w[b, c] for c in range(5)])
+                for c in range(5):
+                    out[a, b, c, part, :] = total[b, c] + y[c]
+            return carry
+
+        lax.fori_loop(0, 5 * halves, plane, 0)
+
+        def columns(i, carry):
+            b = lax.rem(i, 5)
+            part = pl.ds(pl.multiple_of((i // 5) * 8, 8), 8)
+            for c in range(5):
+                y = line_terms(
+                    [expanded[a, b, c, part, :] for a in range(5)],
+                    [weighted[a, b, c, part, :] for a in range(5)],
+                )
+                for a in range(5):
+                    out[a, b, c, part, :] += y[a]
+            return carry
+
+        lax.fori_loop(0, 5 * halves, columns, 0)
+        fold(4, get_from(out), put_in(out))
+
+    def iteration(_, rho_old):
+        precondition()
+        total = jnp.zeros((rows, lanes), jnp.float32)
+        for k in phases(4):
+            r = resid[k]
+            z = guess[k] + winv[k] * (r - out[k])
+            guess[k] = z
+            total = total + r * z
+        rho = jnp.sum(total, axis=(0, 1), keepdims=True)
+        beta = rho / rho_old
+        for k in phases(4):
+            p = guess[k] + beta * direction[k]
+            direction[k] = p
+            expanded[k] = p
+        operator()
+        total = jnp.zeros((rows, lanes), jnp.float32)
+        for k in phases(4):
+            total = total + direction[k] * out[k]
+        alpha = rho / jnp.sum(total, axis=(0, 1), keepdims=True)
+        for k in phases(4):
+            iterate[k] += alpha * direction[k]
+            resid[k] -= masked(*k, alpha * out[k])
+        return rho
+
+    lax.fori_loop(0, 2, iteration, jnp.ones((1, 1), jnp.float32))
+
+    base = where_ref[0]
+    for field, result in ((iterate, solution_ref), (resid, residual_ref)):
+        for a in range(1, 5):
+            for b in range(1, 5):
+                at = lax.rem(base + (a // 4) * ny + b // 4, rows)
+                for c in range(4):
+                    slot = (c + 3) % 4
+                    result[slot, pl.ds(4 * (a - 1) + b - 1, 1), :] = field[
+                        a % 4, b % 4, c, pl.ds(at, 1), :
+                    ]
+        result[3] = next_z(result[3])
+
+
+def replicated_body(kappa, source):
+    local = kappa.shape[5]
+
+    def gathered(t):
+        flat = t.reshape(125, local)
+        whole = lax.all_gather(flat, ("gx", "gy", "gz"))
+        nx, ny, nz = (lax.axis_size(name) for name in ("gx", "gy", "gz"))
+        whole = whole.reshape(nx * ny, nz, 125, local)
+        return jnp.transpose(whole, (2, 0, 1, 3)).reshape(5, 5, 5, nx * ny, nz * local)
+
+    ny = lax.axis_size("gy")
+    kappa, source = gathered(kappa), gathered(source)
+    rows, lanes = kappa.shape[3:]
+    where = (lax.axis_index("gx") * ny + lax.axis_index("gy")).reshape(1).astype(jnp.int32)
+    vmem = pl.BlockSpec(memory_space=pltpu.VMEM)
+
+    def field(n):
+        return pltpu.VMEM((n, n, n, rows, lanes), jnp.float32)
+
+    outs = pl.pallas_call(
+        lambda *refs: replicated_kernel(ny, *refs),
+        out_shape=[jax.ShapeDtypeStruct((4, 16, lanes), jnp.float32)] * 2,
+        in_specs=[pl.BlockSpec(memory_space=pltpu.SMEM), vmem, vmem],
+        out_specs=[vmem, vmem],
+        scratch_shapes=[field(5), field(5), field(5)] + [field(4)] * 6,
+        name="replicated",
+    )(where, kappa, source)
+
+    def own(t):
+        t = lax.dynamic_slice_in_dim(t, lax.axis_index("gz") * local, local, axis=2)
+        return jnp.transpose(t, (1, 2, 0)).reshape(4, 4, 4 * local)
+
+    return own(outs[0]), own(outs[1])
+
+
+def body(kappa, source):
+    nx, ny, nz = (lax.axis_size(name) for name in ("gx", "gy", "gz"))
+    local_x, local_y, local_z = kappa.shape[3:]
+    rows, lanes = nx * local_x * ny * local_y, nz * local_z
+    small = rows % 8 == 0 and lanes % 128 == 0 and rows * lanes <= 8192
+    if local_x == 1 and local_y == 1 and small:
+        return replicated_body(kappa, source)
+    return distributed_body(kappa, source)
+
+
 def solution(mesh):
     placed = (P(None, None, None, "gx", "gy", "gz"), P(None, None, None, "gx", "gy", "gz"))
     return jax.shard_map(

time: 480 us -> 175 us (0.36)
  starting transfers between devices: 172 us -> 0 us
  waiting for transfers between devices: 169 us -> 0 us
  blocking collectives: 76.6 us -> 147 us
  other arithmetic: 17.6 us -> 0 us
  local copies, waits for them, and re-layouts: 27.5 us -> 13.2 us
  Pallas kernels: 0 us -> 13.5 us
  between operations: 10.6 us -> 0.67 us
    ppermute x96 -> x0, starting transfers between devices: 172 us -> none  [the longest x48 109 us: extended(): lax.ppermute(tail, axis, [(i, (i + 1) % count) for i in range(ends)])]
    ppermute x96 -> x0, waiting for transfers between devices: 169 us -> none  [the longest x48 167 us: extended(): lax.ppermute(head, axis, [((i + 1) % count, i) for i in range(ends)])]
    all_gather x0 -> x2, blocking collectives: none -> 147 us  [gathered(): whole = lax.all_gather(flat, ('gx', 'gy', 'gz'))]
    psum x2 -> x0, blocking collectives: 76.6 us -> none  [inner_pair(): return lax.psum((local_rho, local_curv), ('gx', 'gy', 'gz'))]
    pallas_call x0 -> x1, Pallas kernels: none -> 13.5 us  [replicated_body(): pl.pallas_call(lambda *refs: replicated_kernel(ny, *refs), out_shape=[jax...]
    unnamed x38 -> x0, local copies, waits for them, and re-layouts: 8.17 us -> none
    slice x93 -> x0, local copies, waits for them, and re-layouts: 8.07 us -> none  [the longest x11 1.84 us: prolong_first(): return jnp.concatenate([woven, coarse[-1:]], axis=0)]
    add x89 -> x0, other arithmetic: 4.92 us -> none  [the longest x47 2 us: collapse_leading(): head = inner[0] + padded[0]]
  transfers between devices with their start and end apart: 96 -> 0, of which waited for: 54 -> 0; matrix products, arithmetic and copies ran while one was open for 1% -> 0% of each run, Pallas kernels for 0% -> 0%
where the time goes in v1:
time: 175 us
  blocking collectives  147 us (84%)
  Pallas kernels  13.5 us (8%)
  local copies, waits for them, and re-layouts  13.2 us (8%)
    all_gather x2, blocking collectives, gathered(): whole = lax.all_gather(flat, ('gx', 'gy', 'gz'))  147 us
    pallas_call x1, Pallas kernels, replicated_body(): pl.pallas_call(lambda *refs: replicated_kernel(ny, *refs), out_shape=[jax...  13.5 us
    reshape x2, local copies, waits for them, and re-layouts, gathered(): jnp.transpose(whole, (2, 0, 1, 3)).reshape(5, 5, 5, nx * ny, nz * local)  4.26 us
    reshape x2, local copies, waits for them, and re-layouts, gathered(): whole = whole.reshape(nx * ny, nz, 125, local)  3.92 us

profile of v1, /device:TPU:0, one launch (start us, length us, event | category | flops | bytes accessed | tf_op | source)
XLA Modules:
  0.0 174.6 jit_solution(1879807990345793887)
XLA Ops:
  0.6 0.9 copy.12
  1.5 0.9 copy.14
  2.5 76.1 %all_gather.7 = f32[32,125,64]{1,2,0:T(8,128)S(1)} all-gather(f32[1,125,64]{1,2,0:T(8,128)S(1)} %copy.14), channel_id=1, replica_groups=mesh['gx'=4,'gy'=4,'gz'=2] {'gx','gy','gz'}, dimensions={0}, use_global_device_ids=true | all-gather | bytes 1056000 | tf_op jit(solution)/shard_map/all_gather | solution.py:762
  78.6 2.0 %copy.15 = f32[16,2,125,64]{3,1,0,2:T(2,128)S(1)} copy(f32[16,2,125,64]{2,3,1,0:T(8,128)S(1)} %bitcast.13) | data formatting | bytes 2048000 | tf_op jit(solution)/shard_map/reshape | solution.py:764
  80.5 2.2 %reshape.29.refs_2_ = f32[5,5,5,16,128]{4,3,2,1,0:T(8,128)} reshape(f32[125,16,2,64]{3,2,1,0:T(2,128)S(1)} %bitcast.11) | data formatting | bytes 2048000 | tf_op jit(solution)/shard_map/reshape | solution.py:765
  82.7 71.2 %all_gather.6 = f32[32,125,64]{1,2,0:T(8,128)S(1)} all-gather(f32[1,125,64]{1,2,0:T(8,128)S(1)} %copy.12), channel_id=1, replica_groups=mesh['gx'=4,'gy'=4,'gz'=2] {'gx','gy','gz'}, dimensions={0}, use_global_device_ids=true | all-gather | bytes 1056000 | tf_op jit(solution)/shard_map/all_gather | solution.py:762
  153.9 2.0 %copy.13 = f32[16,2,125,64]{3,1,0,2:T(2,128)S(1)} copy(f32[16,2,125,64]{2,3,1,0:T(8,128)S(1)} %bitcast.14) | data formatting | bytes 2048000 | tf_op jit(solution)/shard_map/reshape | solution.py:764
  155.9 2.1 %reshape.27.refs_1_ = f32[5,5,5,16,128]{4,3,2,1,0:T(8,128)} reshape(f32[125,16,2,64]{3,2,1,0:T(2,128)S(1)} %bitcast.12) | data formatting | bytes 2048000 | tf_op jit(solution)/shard_map/reshape | solution.py:765
  158.0 13.5 %replicated.1 = (f32[4,16,128]{2,1,0:T(8,128)}, f32[4,16,128]{2,1,0:T(8,128)}) custom-call(s32[1]{0:T(128)} %bitcast.refs_0_, f32[5,5,5,16,128]{4,3,2,1,0:T(8,128)} %reshape.27.refs_1_, f32[5,5,5,16,128]{4,3,2,1,0:T(8,128)} %reshape.29.refs_2_), custom_call_target="tpu_custom_call" | custom-call | tf_op jit(solution)/shard_map/replicated/pallas_call | solution.py:776
  171.5 0.9 dynamic-slice_bitcast_fusion
  172.3 0.2 copy.17
  172.6 0.9 reshape.31
  173.5 0.2 copy.16
  173.7 0.9 reshape.30

commit v2 on v1

--- a/solution.py
+++ b/solution.py
@@ -415,10 +415,10 @@
 
 
 def replicated_kernel(
-    ny, where_ref, kappa_ref, source_ref, solution_ref, residual_ref,
+    ny, where_ref, blocks_ref, solution_ref, residual_ref,
     weighted, expanded, out, coeff, winv, resid, guess, direction, iterate,
 ):
-    rows, lanes = kappa_ref.shape[3:]
+    rows, lanes = weighted.shape[3:]
     halves = rows // 8
 
     def next_x(t):
@@ -487,25 +487,27 @@
     def get_from(ref):
         return lambda k: ref[k]
 
+    first = lane < lanes // 2
     for a in range(5):
         for b in range(5):
             for c in range(5):
                 w = float(QUAD[a] * QUAD[b] * QUAD[c])
-                weighted[a, b, c] = w * kappa_ref[a, b, c]
-                out[a, b, c] = w * source_ref[a, b, c]
+                both = blocks_ref[:, (a * 5 + b) * 5 + c, :]
+                lower, higher = both[:rows], both[rows:]
+                kappa = jnp.where(first, lower, pltpu.roll(higher, lanes // 2, 1))
+                source = jnp.where(first, pltpu.roll(lower, lanes // 2, 1), higher)
+                expanded[a, b, c] = kappa
+                weighted[a, b, c] = w * kappa
+                out[a, b, c] = w * source
     fold(4, get_from(out), put_in(out))
     for k in phases(4):
         resid[k] = masked(*k, out[k])
         direction[k] = jnp.zeros((rows, lanes), jnp.float32)
         iterate[k] = jnp.zeros((rows, lanes), jnp.float32)
 
-    def pair_z(h):
-        i, _ = h
-        return i
-
     for a in range(4):
         two = {
-            (b, c): kappa_ref[a, b, c] + kappa_ref[a + 1, b, c]
+            (b, c): expanded[a, b, c] + expanded[a + 1, b, c]
             for b in range(5) for c in range(5)
         }
         two = {(b, c): two[b, c] + two[b + 1, c] for b in range(4) for c in range(5)}
@@ -754,21 +756,109 @@
         result[3] = next_z(result[3])
 
 
+def gather_kernel(block_ref, all_ref, own_sem, send_sem, recv_sem):
+    gx, gy, gz = (lax.axis_index(name) for name in ("gx", "gy", "gz"))
+    nx, ny = lax.axis_size("gx"), lax.axis_size("gy")
+    rows = block_ref.shape[0]
+    upper = rows // 16 * 8
+    mesh_id = pl.DeviceIdType.MESH
+    cross_x = lax.rem(gx + 2, nx)
+    twin = gx + 1 - 2 * lax.rem(gx, 2)
+    cross_z = 1 - gz
+    to_x, to_z, to_twin = (cross_x, gy, gz), (gx, gy, cross_z), (twin, gy, gz)
+    to_y = [(gx, lax.rem(gy + d, ny), gz) for d in range(1, ny)]
+
+    barrier = pltpu.get_barrier_semaphore()
+    peers = to_y + [to_x, to_z, to_twin]
+    for peer in peers:
+        pl.semaphore_signal(barrier, inc=1, device_id=peer, device_id_type=mesh_id)
+    pl.semaphore_wait(barrier, len(peers))
+
+    def slot(z, x, y):
+        return (z * nx + x) * ny + y
+
+    started = []
+
+    def send(src, dst, device):
+        number = len(started)
+        copy = pltpu.make_async_remote_copy(
+            src_ref=src,
+            dst_ref=dst,
+            send_sem=send_sem.at[number],
+            recv_sem=recv_sem.at[number],
+            device_id=device,
+            device_id_type=mesh_id,
+        )
+        copy.start()
+        started.append(copy)
+        return copy
+
+    mine = all_ref.at[slot(gz, gx, gy)]
+    along = [None] + [send(block_ref, mine, device) for device in to_y]
+    own = pltpu.make_async_copy(block_ref, mine, own_sem)
+    own.start()
+    ys = [lax.rem(gy + ny - d, ny) for d in range(ny)]
+    by_x, by_z, by_xz, by_zx, last = {}, {}, {}, {}, []
+
+    def column(d):
+        if d:
+            along[d].wait_recv()
+        here = all_ref.at[slot(gz, gx, ys[d])]
+        src = here if d else block_ref
+        by_x[d] = send(src, here, to_x)
+        by_z[d] = send(src, here, to_z)
+        last.append(send(src, here, to_twin))
+
+    def onward(d):
+        by_x[d].wait_recv()
+        number = slot(gz, cross_x, ys[d])
+        part = all_ref.at[number, pl.ds(0, upper)]
+        by_xz[d] = send(part, part, to_z)
+        last.append(send(all_ref.at[number], all_ref.at[number], to_twin))
+        by_z[d].wait_recv()
+        number = slot(cross_z, gx, ys[d])
+        part = all_ref.at[number, pl.ds(upper, rows - upper)]
+        by_zx[d] = send(part, part, to_x)
+        last.append(send(all_ref.at[number], all_ref.at[number], to_twin))
+
+    column(0)
+    for d in range(1, ny):
+        column(d)
+        onward(d - 1)
+    onward(ny - 1)
+    for d in range(ny):
+        by_xz[d].wait_recv()
+        by_zx[d].wait_recv()
+        here = all_ref.at[slot(cross_z, cross_x, ys[d])]
+        last.append(send(here, here, to_twin))
+    for copy in last:
+        copy.wait_recv()
+    own.wait()
+    for copy in started:
+        copy.wait_send()
+
+
 def replicated_body(kappa, source):
     local = kappa.shape[5]
-
-    def gathered(t):
-        flat = t.reshape(125, local)
-        whole = lax.all_gather(flat, ("gx", "gy", "gz"))
-        nx, ny, nz = (lax.axis_size(name) for name in ("gx", "gy", "gz"))
-        whole = whole.reshape(nx * ny, nz, 125, local)
-        return jnp.transpose(whole, (2, 0, 1, 3)).reshape(5, 5, 5, nx * ny, nz * local)
-
-    ny = lax.axis_size("gy")
-    kappa, source = gathered(kappa), gathered(source)
-    rows, lanes = kappa.shape[3:]
+    nx, ny, nz = (lax.axis_size(name) for name in ("gx", "gy", "gz"))
+    vmem = pl.BlockSpec(memory_space=pltpu.VMEM)
+    block = jnp.concatenate([kappa.reshape(125, local), source.reshape(125, local)], axis=1)
+    copies = (ny - 1) + 8 * ny
+    blocks = pl.pallas_call(
+        gather_kernel,
+        out_shape=jax.ShapeDtypeStruct((nz * nx * ny,) + block.shape, jnp.float32),
+        in_specs=[vmem],
+        out_specs=vmem,
+        scratch_shapes=[
+            pltpu.SemaphoreType.DMA,
+            pltpu.SemaphoreType.DMA((copies,)),
+            pltpu.SemaphoreType.DMA((copies,)),
+        ],
+        compiler_params=pltpu.CompilerParams(collective_id=0, has_side_effects=True),
+        name="gather",
+    )(block)
+    rows, lanes = nx * ny, nz * local
     where = (lax.axis_index("gx") * ny + lax.axis_index("gy")).reshape(1).astype(jnp.int32)
-    vmem = pl.BlockSpec(memory_space=pltpu.VMEM)
 
     def field(n):
         return pltpu.VMEM((n, n, n, rows, lanes), jnp.float32)
@@ -776,11 +866,11 @@
     outs = pl.pallas_call(
         lambda *refs: replicated_kernel(ny, *refs),
         out_shape=[jax.ShapeDtypeStruct((4, 16, lanes), jnp.float32)] * 2,
-        in_specs=[pl.BlockSpec(memory_space=pltpu.SMEM), vmem, vmem],
+        in_specs=[pl.BlockSpec(memory_space=pltpu.SMEM), vmem],
         out_specs=[vmem, vmem],
         scratch_shapes=[field(5), field(5), field(5)] + [field(4)] * 6,
         name="replicated",
-    )(where, kappa, source)
+    )(where, blocks)
 
     def own(t):
         t = lax.dynamic_slice_in_dim(t, lax.axis_index("gz") * local, local, axis=2)
@@ -792,9 +882,9 @@
 def body(kappa, source):
     nx, ny, nz = (lax.axis_size(name) for name in ("gx", "gy", "gz"))
     local_x, local_y, local_z = kappa.shape[3:]
-    rows, lanes = nx * local_x * ny * local_y, nz * local_z
-    small = rows % 8 == 0 and lanes % 128 == 0 and rows * lanes <= 8192
-    if local_x == 1 and local_y == 1 and small:
+    rows, lanes = nx * ny, nz * local_z
+    small = rows % 8 == 0 and lanes == 128 and rows <= 64
+    if local_x == 1 and local_y == 1 and nx == 4 and nz == 2 and small:
         return replicated_body(kappa, source)
     return distributed_body(kappa, source)
 

time: 175 us -> 46.3 us (0.26)
  blocking collectives: 147 us -> 0 us
  Pallas kernels: 13.5 us -> 39.3 us
  local copies, waits for them, and re-layouts: 13.2 us -> 3.18 us
  other arithmetic: 0 us -> 2.71 us
    all_gather x2 -> x0, blocking collectives: 147 us -> none  [gathered(): whole = lax.all_gather(flat, ('gx', 'gy', 'gz'))]
    pallas_call x0 -> x1, Pallas kernels: none -> 24.4 us  [replicated_body(): pl.pallas_call(gather_kernel, out_shape=jax.ShapeDtypeStruct((nz * nx * n...]
    reshape x4 -> x2, local copies, waits for them, and re-layouts: 8.18 us -> 0.02 us  [the longest x1 0.01 us: replicated_body(): kappa.reshape(125, local)]
    unnamed x0 -> x2, other arithmetic: none -> 2 us
    another operation x2 -> x0, local copies, waits for them, and re-layouts: 1.82 us -> none  [gathered(): whole = lax.all_gather(flat, ('gx', 'gy', 'gz'))]
where the time goes in v2:
time: 46.3 us; the launch traced here: 45.9 us
  Pallas kernels  39.3 us (85%)
  local copies, waits for them, and re-layouts  3.18 us (7%)
  other arithmetic  2.71 us (6%)
  between operations  0.68 us (1%)
    pallas_call x1, Pallas kernels, replicated_body(): pl.pallas_call(gather_kernel, out_shape=jax.ShapeDtypeStruct((nz * nx * n...  24.4 us
    pallas_call x1, Pallas kernels, replicated_body(): pl.pallas_call(lambda *refs: replicated_kernel(ny, *refs), out_shape=[jax...  14.9 us
    unnamed x2, other arithmetic  2 us
    reshape x2, local copies, waits for them, and re-layouts, own(): return jnp.transpose(t, (1, 2, 0)).reshape(4, 4, 4 * local)  1.82 us
    transpose x3, local copies, waits for them, and re-layouts, own(): return jnp.transpose(t, (1, 2, 0)).reshape(4, 4, 4 * local)  1.34 us

profile of v2, /device:TPU:0, one launch (start us, length us, event | category | flops | bytes accessed | tf_op | source)
XLA Modules:
  0.0 45.9 jit_solution(7644053369969472573)
XLA Ops:
  0.6 1.0 %reduce = f32[5,5,5,64]{3,2,1,0:T(8,128)S(1)} reduce(f32[5,5,5,1,1,64]{5,4,3,2,1,0:T(1,128)} %param.2, f32[]{:T(128)} %constant.21), dimensions={3,4}, to_apply=%param.2.reduce_sub_computation | reduce | bytes 64004 | tf_op args[0]
  1.7 1.0 %reduce.1 = f32[5,5,5,64]{3,2,1,0:T(8,128)S(1)} reduce(f32[5,5,5,1,1,64]{5,4,3,2,1,0:T(1,128)} %param.3, f32[]{:T(128)} %constant.21), dimensions={3,4}, to_apply=%param.3.reduce_sub_computation | reduce | bytes 64004 | tf_op args[1]
  2.7 0.7 %pad_maximum_fusion.block_ref = f32[125,128]{1,0:T(8,128)} fusion(f32[125,64]{1,0:T(8,128)S(1)} %reshape.21, f32[125,64]{1,0:T(8,128)S(1)} %reshape.20), kind=kLoop, calls=%fused_computation | loop fusion | flops 16000 | bytes 128000 | tf_op jit(solution)/shard_map/concatenate | solution.py:845
  3.4 24.4 %gather.1.refs_1_ = f32[32,125,128]{2,1,0:T(8,128)} custom-call(f32[125,128]{1,0:T(8,128)} %pad_maximum_fusion.block_ref), custom_call_target="tpu_custom_call" | custom-call | tf_op jit(solution)/shard_map/gather/pallas_call | solution.py:847
  27.8 14.9 %replicated.1 = (f32[4,16,128]{2,1,0:T(8,128)}, f32[4,16,128]{2,1,0:T(8,128)}) custom-call(s32[1]{0:T(128)} %bitcast.refs_0_, f32[32,125,128]{2,1,0:T(8,128)} %gather.1.refs_1_), custom_call_target="tpu_custom_call" | custom-call | tf_op jit(solution)/shard_map/replicated/pallas_call | solution.py:866
  42.7 0.9 %dynamic-slice_bitcast_fusion = (f32[16,64,4]{1,0,2:T(8,128)S(1)}, f32[16,64,4]{1,0,2:T(8,128)S(1)}) fusion(f32[4,16,128]{2,1,0:T(8,128)} %get-tuple-element.5, s32[]{:T(128)S(6)} %select_n.4, f32[4,16,128]{2,1,0:T(8,128)} %get-tuple-element.4), kind=kLoop, calls=%fused_computation.1 | loop fusion | bytes 65540 | tf_op jit(solution)/shard_map/transpose | solution.py:877
  43.6 0.2 copy.5
  43.8 0.9 %reshape.23 = f32[4,4,256]{2,1,0:T(4,128)} reshape(f32[16,64,4]{2,1,0:T(8,128)S(1)} %copy.5) | data formatting | bytes 32768 | tf_op jit(solution)/shard_map/reshape | solution.py:877
  44.7 0.2 copy.4
  45.0 0.9 %reshape.22 = f32[4,4,256]{2,1,0:T(4,128)} reshape(f32[16,64,4]{2,1,0:T(8,128)S(1)} %copy.4) | data formatting | bytes 32768 | tf_op jit(solution)/shard_map/reshape | solution.py:877
  (2 shorter events, 0.0 us)

commit v3 on v2

--- a/solution.py
+++ b/solution.py
@@ -416,7 +416,7 @@
 
 def replicated_kernel(
     ny, where_ref, blocks_ref, solution_ref, residual_ref,
-    weighted, expanded, out, coeff, winv, resid, guess, direction, iterate,
+    weighted, expanded, out, coeff, winv, resid, guess, direction, iterate, picked,
 ):
     rows, lanes = weighted.shape[3:]
     halves = rows // 8
@@ -744,16 +744,33 @@
     lax.fori_loop(0, 2, iteration, jnp.ones((1, 1), jnp.float32))
 
     base = where_ref[0]
-    for field, result in ((iterate, solution_ref), (resid, residual_ref)):
+    for index, field in enumerate((iterate, resid)):
         for a in range(1, 5):
             for b in range(1, 5):
                 at = lax.rem(base + (a // 4) * ny + b // 4, rows)
                 for c in range(4):
-                    slot = (c + 3) % 4
-                    result[slot, pl.ds(4 * (a - 1) + b - 1, 1), :] = field[
+                    picked[c, pl.ds(16 * index + 4 * (a - 1) + b - 1, 1), :] = field[
                         a % 4, b % 4, c, pl.ds(at, 1), :
                     ]
-        result[3] = next_z(result[3])
+    width = solution_ref.shape[2]
+    lane_in = lax.broadcasted_iota(jnp.int32, (lanes, width), 0)
+    lane_out = lax.broadcasted_iota(jnp.int32, (lanes, width), 1)
+    total = jnp.zeros((32, width), jnp.float32)
+    for slot in range(4):
+        t = picked[1 + slot] if slot < 3 else next_z(picked[0])
+        hot = (lane_out == 4 * (lane_in - where_ref[1]) + slot).astype(jnp.bfloat16)
+        high = t.astype(jnp.bfloat16)
+        rest = t - high.astype(jnp.float32)
+        middle = rest.astype(jnp.bfloat16)
+        low = (rest - middle.astype(jnp.float32)).astype(jnp.bfloat16)
+        parts = jnp.dot(
+            jnp.concatenate([high, middle, low], axis=0), hot,
+            preferred_element_type=jnp.float32,
+        )
+        total = total + ((parts[:32] + parts[32:64]) + parts[64:])
+    for i in range(4):
+        solution_ref[i] = total[4 * i : 4 * i + 4]
+        residual_ref[i] = total[16 + 4 * i : 20 + 4 * i]
 
 
 def gather_kernel(block_ref, all_ref, own_sem, send_sem, recv_sem):
@@ -842,11 +859,11 @@
     local = kappa.shape[5]
     nx, ny, nz = (lax.axis_size(name) for name in ("gx", "gy", "gz"))
     vmem = pl.BlockSpec(memory_space=pltpu.VMEM)
-    block = jnp.concatenate([kappa.reshape(125, local), source.reshape(125, local)], axis=1)
+    block = jnp.concatenate([kappa, source], axis=5).reshape(125, 2 * local)
     copies = (ny - 1) + 8 * ny
     blocks = pl.pallas_call(
         gather_kernel,
-        out_shape=jax.ShapeDtypeStruct((nz * nx * ny,) + block.shape, jnp.float32),
+        out_shape=pltpu.VMEM((nz * nx * ny,) + block.shape, jnp.float32),
         in_specs=[vmem],
         out_specs=vmem,
         scratch_shapes=[
@@ -858,25 +875,23 @@
         name="gather",
     )(block)
     rows, lanes = nx * ny, nz * local
-    where = (lax.axis_index("gx") * ny + lax.axis_index("gy")).reshape(1).astype(jnp.int32)
+    place = lax.axis_index("gx") * ny + lax.axis_index("gy")
+    where = jnp.stack([place, lax.axis_index("gz") * local]).astype(jnp.int32)
 
     def field(n):
         return pltpu.VMEM((n, n, n, rows, lanes), jnp.float32)
 
     outs = pl.pallas_call(
         lambda *refs: replicated_kernel(ny, *refs),
-        out_shape=[jax.ShapeDtypeStruct((4, 16, lanes), jnp.float32)] * 2,
+        out_shape=[jax.ShapeDtypeStruct((4, 4, 4 * local), jnp.float32)] * 2,
         in_specs=[pl.BlockSpec(memory_space=pltpu.SMEM), vmem],
         out_specs=[vmem, vmem],
-        scratch_shapes=[field(5), field(5), field(5)] + [field(4)] * 6,
+        scratch_shapes=[field(5), field(5), field(5)] + [field(4)] * 6
+        + [pltpu.VMEM((4, 32, lanes), jnp.float32)],
         name="replicated",
-    )(where, blocks)
-
-    def own(t):
-        t = lax.dynamic_slice_in_dim(t, lax.axis_index("gz") * local, local, axis=2)
-        return jnp.transpose(t, (1, 2, 0)).reshape(4, 4, 4 * local)
-
-    return own(outs[0]), own(outs[1])
+    )(where, pltpu.with_memory_space_constraint(blocks, pltpu.VMEM))
+
+    return outs[0], outs[1]
 
 
 def body(kappa, source):

time: 46.3 us -> 40.5 us (0.87)
  local copies, waits for them, and re-layouts: 3.18 us -> 0.63 us
  Pallas kernels: 39.3 us -> 37.3 us
  other arithmetic: 2.71 us -> 1.75 us
    unnamed x2 -> x0, other arithmetic: 2 us -> none
    pallas_call x1, Pallas kernels: 24.4 us -> 23.1 us  [replicated_body(): pl.pallas_call(gather_kernel, out_shape=pltpu.VMEM((nz * nx * ny,) + bloc...]
    transpose x3 -> x0, local copies, waits for them, and re-layouts: 1.34 us -> none  [own(): return jnp.transpose(t, (1, 2, 0)).reshape(4, 4, 4 * local)]
    reshape x4 -> x1, local copies, waits for them, and re-layouts: 1.84 us -> 0.63 us  [replicated_body(): block = jnp.concatenate([kappa, source], axis=5).reshape(125, 2 * local)]
    pallas_call x1, Pallas kernels: 14.9 us -> 14.2 us  [replicated_body(): pl.pallas_call(lambda *refs: replicated_kernel(ny, *refs), out_shape=[jax...]
    another operation x0 -> x1, other arithmetic: none -> 0.62 us  [replicated_body(): where = jnp.stack([place, lax.axis_index('gz') * local]).astype(jnp.int32)]
where the time goes in v3:
time: 40.5 us; the launch traced here: 40.3 us
  Pallas kernels  37.3 us (92%)
  other arithmetic  1.75 us (4%)
  between operations  0.65 us (2%)
  local copies, waits for them, and re-layouts  0.63 us (2%)
    pallas_call x1, Pallas kernels, replicated_body(): pl.pallas_call(gather_kernel, out_shape=pltpu.VMEM((nz * nx * ny,) + bloc...  23.1 us
    pallas_call x1, Pallas kernels, replicated_body(): pl.pallas_call(lambda *refs: replicated_kernel(ny, *refs), out_shape=[jax...  14.2 us
    concatenate x1, other arithmetic, replicated_body(): block = jnp.concatenate([kappa, source], axis=5).reshape(125, 2 * local)  1.13 us

profile of v3, /device:TPU:0, one launch (start us, length us, event | category | flops | bytes accessed | tf_op | source)
XLA Modules:
  0.0 40.3 jit_solution(6333028674746602098)
XLA Ops:
  0.6 0.6 %pad_add_fusion.refs_0_ = s32[2]{0:T(128)} fusion(s32[1]{0:T(128)} %bitcast.1, s32[1]{0:T(128)} %bitcast), kind=kLoop, calls=%fused_computation.1 | loop fusion | flops 2 | bytes 16 | tf_op jit(solution)/shard_map/stack | solution.py:879
  1.3 1.1 %maximum_reduce_fusion = f32[5,5,5,128]{3,2,1,0:T(8,128)S(1)} fusion(f32[5,5,5,1,1,64]{5,4,3,2,1,0:T(1,128)} %param.3, f32[5,5,5,1,1,64]{5,4,3,2,1,0:T(1,128)} %param.2), kind=kLoop, calls=%fused_computation | loop fusion | flops 16000 | bytes 128000 | tf_op jit(solution)/shard_map/concatenate | solution.py:862
  2.4 0.6 %reshape.7.block_ref = f32[125,128]{1,0:T(8,128)} reshape(f32[5,5,5,128]{3,2,1,0:T(8,128)S(1)} %maximum_reduce_fusion) | data formatting | bytes 128000 | tf_op jit(solution)/shard_map/reshape | solution.py:862
  3.0 23.1 %gather.1.refs_1_ = f32[32,125,128]{2,1,0:T(8,128)S(1)} custom-call(f32[125,128]{1,0:T(8,128)} %reshape.7.block_ref), custom_call_target="tpu_custom_call" | custom-call | tf_op jit(solution)/shard_map/gather/pallas_call | solution.py:864
  26.1 14.2 %replicated.1 = (f32[4,4,256]{2,1,0:T(4,128)}, f32[4,4,256]{2,1,0:T(4,128)}) custom-call(s32[2]{0:T(128)} %pad_add_fusion.refs_0_, f32[32,125,128]{2,1,0:T(8,128)S(1)} %gather.1.refs_1_), custom_call_target="tpu_custom_call" | custom-call | tf_op jit(solution)/shard_map/replicated/pallas_call | solution.py:884

commit v4 on v3

--- a/solution.py
+++ b/solution.py
@@ -415,7 +415,7 @@
 
 
 def replicated_kernel(
-    ny, where_ref, blocks_ref, solution_ref, residual_ref,
+    ny, local, blocks_ref, solution_ref, residual_ref,
     weighted, expanded, out, coeff, winv, resid, guess, direction, iterate, picked,
 ):
     rows, lanes = weighted.shape[3:]
@@ -743,7 +743,8 @@
 
     lax.fori_loop(0, 2, iteration, jnp.ones((1, 1), jnp.float32))
 
-    base = where_ref[0]
+    base = lax.axis_index("gx") * ny + lax.axis_index("gy")
+    start = lax.axis_index("gz") * local
     for index, field in enumerate((iterate, resid)):
         for a in range(1, 5):
             for b in range(1, 5):
@@ -758,7 +759,7 @@
     total = jnp.zeros((32, width), jnp.float32)
     for slot in range(4):
         t = picked[1 + slot] if slot < 3 else next_z(picked[0])
-        hot = (lane_out == 4 * (lane_in - where_ref[1]) + slot).astype(jnp.bfloat16)
+        hot = (lane_out == 4 * (lane_in - start) + slot).astype(jnp.bfloat16)
         high = t.astype(jnp.bfloat16)
         rest = t - high.astype(jnp.float32)
         middle = rest.astype(jnp.bfloat16)
@@ -773,6 +774,15 @@
         residual_ref[i] = total[16 + 4 * i : 20 + 4 * i]
 
 
+def flipped(index, bits):
+    step = 1
+    while step <= bits:
+        if bits & step:
+            index = index + step - 2 * step * lax.rem(index // step, 2)
+        step *= 2
+    return index
+
+
 def gather_kernel(block_ref, all_ref, own_sem, send_sem, recv_sem):
     gx, gy, gz = (lax.axis_index(name) for name in ("gx", "gy", "gz"))
     nx, ny = lax.axis_size("gx"), lax.axis_size("gy")
@@ -783,7 +793,8 @@
     twin = gx + 1 - 2 * lax.rem(gx, 2)
     cross_z = 1 - gz
     to_x, to_z, to_twin = (cross_x, gy, gz), (gx, gy, cross_z), (twin, gy, gz)
-    to_y = [(gx, lax.rem(gy + d, ny), gz) for d in range(1, ny)]
+    ys = [flipped(gy, d) for d in range(ny)]
+    to_y = [(gx, y, gz) for y in ys[1:]]
 
     barrier = pltpu.get_barrier_semaphore()
     peers = to_y + [to_x, to_z, to_twin]
@@ -814,7 +825,6 @@
     along = [None] + [send(block_ref, mine, device) for device in to_y]
     own = pltpu.make_async_copy(block_ref, mine, own_sem)
     own.start()
-    ys = [lax.rem(gy + ny - d, ny) for d in range(ny)]
     by_x, by_z, by_xz, by_zx, last = {}, {}, {}, {}, []
 
     def column(d):
@@ -875,21 +885,19 @@
         name="gather",
     )(block)
     rows, lanes = nx * ny, nz * local
-    place = lax.axis_index("gx") * ny + lax.axis_index("gy")
-    where = jnp.stack([place, lax.axis_index("gz") * local]).astype(jnp.int32)
 
     def field(n):
         return pltpu.VMEM((n, n, n, rows, lanes), jnp.float32)
 
     outs = pl.pallas_call(
-        lambda *refs: replicated_kernel(ny, *refs),
+        lambda *refs: replicated_kernel(ny, local, *refs),
         out_shape=[jax.ShapeDtypeStruct((4, 4, 4 * local), jnp.float32)] * 2,
-        in_specs=[pl.BlockSpec(memory_space=pltpu.SMEM), vmem],
+        in_specs=[vmem],
         out_specs=[vmem, vmem],
         scratch_shapes=[field(5), field(5), field(5)] + [field(4)] * 6
         + [pltpu.VMEM((4, 32, lanes), jnp.float32)],
         name="replicated",
-    )(where, pltpu.with_memory_space_constraint(blocks, pltpu.VMEM))
+    )(pltpu.with_memory_space_constraint(blocks, pltpu.VMEM))
 
     return outs[0], outs[1]
 
@@ -899,7 +907,7 @@
     local_x, local_y, local_z = kappa.shape[3:]
     rows, lanes = nx * ny, nz * local_z
     small = rows % 8 == 0 and lanes == 128 and rows <= 64
-    if local_x == 1 and local_y == 1 and nx == 4 and nz == 2 and small:
+    if local_x == 1 and local_y == 1 and nx == 4 and nz == 2 and ny & (ny - 1) == 0 and small:
         return replicated_body(kappa, source)
     return distributed_body(kappa, source)
 

time: 40.5 us -> 38.2 us (0.943)
  Pallas kernels: 37.3 us -> 35.5 us
  other arithmetic: 1.75 us -> 1.13 us
    pallas_call x1, Pallas kernels: 23.1 us -> 22 us  [replicated_body(): pl.pallas_call(gather_kernel, out_shape=pltpu.VMEM((nz * nx * ny,) + bloc...]
    pallas_call x1, Pallas kernels: 14.2 us -> 13.5 us  [replicated_body(): pl.pallas_call(lambda *refs: replicated_kernel(ny, local, *refs), out_sha...]
    another operation x1 -> x0, other arithmetic: 0.62 us -> none  [replicated_body(): where = jnp.stack([place, lax.axis_index('gz') * local]).astype(jnp.int32)]
where the time goes in v4:
time: 38.2 us; the launch traced here: 37.9 us
  Pallas kernels  35.5 us (93%)
  other arithmetic  1.13 us (3%)
  between operations  0.65 us (2%)
  local copies, waits for them, and re-layouts  0.63 us (2%)
    pallas_call x1, Pallas kernels, replicated_body(): pl.pallas_call(gather_kernel, out_shape=pltpu.VMEM((nz * nx * ny,) + bloc...  22 us
    pallas_call x1, Pallas kernels, replicated_body(): pl.pallas_call(lambda *refs: replicated_kernel(ny, local, *refs), out_sha...  13.5 us
    concatenate x1, other arithmetic, replicated_body(): block = jnp.concatenate([kappa, source], axis=5).reshape(125, 2 * local)  1.13 us

profile of v4, /device:TPU:0, one launch (start us, length us, event | category | flops | bytes accessed | tf_op | source)
XLA Modules:
  0.0 37.9 jit_solution(7328011519422109888)
XLA Ops:
  0.6 1.1 %maximum_reduce_fusion = f32[5,5,5,128]{3,2,1,0:T(8,128)S(1)} fusion(f32[5,5,5,1,1,64]{5,4,3,2,1,0:T(1,128)} %param.3, f32[5,5,5,1,1,64]{5,4,3,2,1,0:T(1,128)} %param.2), kind=kLoop, calls=%fused_computation | loop fusion | flops 16000 | bytes 128000 | tf_op jit(solution)/shard_map/concatenate | solution.py:872
  1.8 0.6 %reshape.7.block_ref = f32[125,128]{1,0:T(8,128)} reshape(f32[5,5,5,128]{3,2,1,0:T(8,128)S(1)} %maximum_reduce_fusion) | data formatting | bytes 128000 | tf_op jit(solution)/shard_map/reshape | solution.py:872
  2.4 22.0 %gather.1.refs_0_ = f32[32,125,128]{2,1,0:T(8,128)S(1)} custom-call(f32[125,128]{1,0:T(8,128)} %reshape.7.block_ref), custom_call_target="tpu_custom_call" | custom-call | tf_op jit(solution)/shard_map/gather/pallas_call | solution.py:874
  24.4 13.5 %replicated.1 = (f32[4,4,256]{2,1,0:T(4,128)}, f32[4,4,256]{2,1,0:T(4,128)}) custom-call(f32[32,125,128]{2,1,0:T(8,128)S(1)} %gather.1.refs_0_), custom_call_target="tpu_custom_call" | custom-call | tf_op jit(solution)/shard_map/replicated/pallas_call | solution.py:892
